TPU v7x, 256 devices: a 8x8x2 block of a 8x8x16 slice. The times are simulated.
256 devices in a mesh: sub: 2 (over z), row: 128 (over y, x, core).
Axes of the slice: x: 8, y: 8, z: 2, core: 2. Of those that a mesh axis runs over, the one named last changes fastest.
The devices are a block of a 8x8x16 slice.
Arguments:
- diag_blocks: float32 [4096, 128, 128], P(('sub', 'row')), parts along dimension 0, may hold values from -0.05 to 16, as said below
- coupling: float32 [4096, 3, 128, 128], P(('sub', 'row')), parts along dimension 0, may hold values from -0.05 to 0.05
- offsets: int32 [4096, 3], P(('sub', 'row')), parts along dimension 0, may hold values from 1 to 4, as said below
- mass: float32 [524288], P(('sub', 'row')), parts along dimension 0, may hold values from 0.5 to 2
- initial_modes: float32 [32, 524288], P(None, ('sub', 'row')), parts along dimension 1, may hold values from -6 to 6
Outputs:
- mass_density: float32 [524288], P(('sub', 'row')), parts along dimension 0
- energy_density: float32 [524288], P(('sub', 'row')), parts along dimension 0
There are 2 independent parts, one for each index of `sub`. A program takes and returns all parts, laid end to end along the dimension named above; each array names one. Nothing has to cross between parts.
Inputs may be any that keep to these rules, and one draw needn't show every extreme that they name: `diag_blocks`: each block is symmetric; entries off a block's diagonal lie in -0.05 to 0.05, its diagonal entries in 1 to 16. The 3 offsets of a block row are distinct.
All inputs are finite; a program needn't handle non-finite values.
Results may differ from a plain program's by a relative error of at most 0.0003.
Values sent between devices are 32-bit elements; how exact they have to be, the bound alone decides.
A program may use at most 128 MiB of HBM per device.

v0:
```python
import jax
import jax.numpy as jnp
from jax import lax
from jax.sharding import Mesh
from jax.sharding import PartitionSpec as P

MODES = 32
REACH = 4
ITERS = 3
PURIFY = 28
ROW = ("row_0", "row_1", "row_2")
SUB_ROW = ("sub", "row_0", "row_1", "row_2")
PRECISE = lax.Precision.HIGHEST


def from_behind(value, axis, steps):
    count = lax.axis_size(axis)
    initial, last = (max(0, -steps), min(count, count - steps))
    return lax.ppermute(value, axis, [(source, source + steps) for source in range(initial, last)])


def one_axis_at_a_time(value, axes):
    for axis in axes:
        value = lax.psum(value, axis)
    return value


def one_hot_table(positions, extent):
    return (positions[..., None] == jnp.arange(extent, dtype=jnp.int32)).astype(jnp.float32)


def stiffness_apply(vectors, diag_blocks, coupling, offsets):
    rowcount = vectors.shape[0]
    block_count = diag_blocks.shape[0]
    block_width = diag_blocks.shape[1]
    blocked = vectors.reshape(rowcount, block_count, block_width)
    result = jnp.einsum("nbk,bkj->nbj", blocked, diag_blocks, precision=PRECISE)
    positions = jnp.arange(block_count, dtype=jnp.int32)[:, None] - offsets + REACH
    products = jnp.einsum("nbk,bskj->nbsj", blocked, coupling, precision=PRECISE)
    lower_part = from_behind(vectors[:, (block_count - REACH) * block_width :], ROW, 1)
    extent = block_count + REACH
    extended = jnp.concatenate([lower_part, vectors], axis=1).reshape(rowcount, extent, block_width)
    selector = one_hot_table(positions, extent)
    gathered = jnp.einsum("bse,nek->nbsk", selector, extended, precision=PRECISE)
    result = result + jnp.einsum("nbsk,bsjk->nbj", gathered, coupling, precision=PRECISE)
    spread = jnp.einsum("bse,nbsj->nej", selector, products, precision=PRECISE)
    returned = from_behind(spread[:, :REACH].reshape(rowcount, REACH * block_width), ROW, -1)
    result = result + spread[:, REACH:]
    result = result.at[:, block_count - REACH :].add(returned.reshape(rowcount, REACH, block_width))
    return result.reshape(rowcount, block_count * block_width)


def purify(matrix, occupied, steps_count):
    order = matrix.shape[0]
    identity = jnp.eye(order, dtype=matrix.dtype)
    diagonal = jnp.diagonal(matrix)
    center = jnp.sum(diagonal) / order
    radius = jnp.sum(jnp.abs(matrix), axis=1) - jnp.abs(diagonal)
    highest = jnp.max(diagonal + radius)
    lowest = jnp.min(diagonal - radius)
    factor = jnp.minimum(
        occupied / jnp.maximum(highest - center, 1e-06),
        (order - occupied) / jnp.maximum(center - lowest, 1e-06),
    )
    initial = factor / order * (center * identity - matrix) + occupied / order * identity

    def purify_step(index, density):
        square = jnp.dot(density, density, precision=PRECISE)
        cube = jnp.dot(square, density, precision=PRECISE)
        numerator = jnp.trace(square - cube)
        denominator = jnp.trace(density - square)
        safe_denominator = jnp.where(jnp.abs(denominator) > 1e-12, denominator, 1.0)
        ratio = jnp.clip(numerator / safe_denominator, 0.0, 1.0)
        upward = ((1.0 + ratio) * square - cube) / jnp.maximum(ratio, 0.5)
        downward = ((1.0 - 2.0 * ratio) * density + (1.0 + ratio) * square - cube) / jnp.maximum(
            1.0 - ratio, 0.5
        )
        return jnp.where(ratio >= 0.5, upward, downward)

    return lax.fori_loop(0, steps_count, purify_step, initial)


def ritz_basis(gram_stiff, gram_mass, modes_wanted, steps_count):
    order = gram_stiff.shape[0]
    gram_stiff = 0.5 * (gram_stiff + gram_stiff.T)
    gram_mass = 0.5 * (gram_mass + gram_mass.T)
    scaling = lax.rsqrt(jnp.diagonal(gram_mass) + 1e-06)
    stiff_scaled = scaling[:, None] * gram_stiff * scaling[None, :]
    mass_scaled = scaling[:, None] * gram_mass * scaling[None, :]
    factor_low = jnp.linalg.cholesky(mass_scaled)
    identity = jnp.eye(order, dtype=gram_stiff.dtype)
    inverse_low = lax.linalg.triangular_solve(factor_low, identity, left_side=True, lower=True)
    reduced = jnp.dot(
        jnp.dot(inverse_low, stiff_scaled, precision=PRECISE), inverse_low.T, precision=PRECISE
    )
    reduced = 0.5 * (reduced + reduced.T)
    if order > modes_wanted:
        projector = purify(reduced, modes_wanted, steps_count)
        columns = projector[:, :modes_wanted]
    else:
        columns = identity
    correlation = jnp.dot(columns.T, columns, precision=PRECISE)
    correlation_low = jnp.linalg.cholesky(correlation)
    orthonormal = lax.linalg.triangular_solve(
        correlation_low, columns.T, left_side=True, lower=True
    ).T
    coefficients = scaling[:, None] * jnp.dot(inverse_low.T, orthonormal, precision=PRECISE)
    projected = jnp.dot(
        jnp.dot(orthonormal.T, reduced, precision=PRECISE), orthonormal, precision=PRECISE
    )
    return (coefficients, 0.5 * (projected + projected.T))


def local(diag_blocks, coupling, offsets, mass, initial_modes):
    stiff_diag = jnp.diagonal(diag_blocks, axis1=1, axis2=2).reshape(-1)

    def gram_pair(basis, stiff_basis):
        local_stiff = jnp.dot(basis, stiff_basis.T, precision=PRECISE)
        local_mass = jnp.dot(basis * mass[None, :], basis.T, precision=PRECISE)
        return (one_axis_at_a_time(local_stiff, ROW), one_axis_at_a_time(local_mass, ROW))

    stiff_initial = stiffness_apply(initial_modes, diag_blocks, coupling, offsets)
    gram_stiff, gram_mass = gram_pair(initial_modes, stiff_initial)
    coefficients, projected = ritz_basis(gram_stiff, gram_mass, MODES, PURIFY)
    modes_now = jnp.dot(coefficients.T, initial_modes, precision=PRECISE)
    stiff_modes = jnp.dot(coefficients.T, stiff_initial, precision=PRECISE)
    directions = None
    stiff_directions = None
    for iteration in range(ITERS):
        residual = stiff_modes - jnp.dot(projected, modes_now * mass[None, :], precision=PRECISE)
        precond = residual / stiff_diag[None, :]
        stiff_precond = stiffness_apply(precond, diag_blocks, coupling, offsets)
        if directions is None:
            basis = jnp.concatenate([modes_now, precond], axis=0)
            stiff_basis = jnp.concatenate([stiff_modes, stiff_precond], axis=0)
        else:
            basis = jnp.concatenate([modes_now, precond, directions], axis=0)
            stiff_basis = jnp.concatenate([stiff_modes, stiff_precond, stiff_directions], axis=0)
        gram_stiff, gram_mass = gram_pair(basis, stiff_basis)
        coefficients, projected = ritz_basis(gram_stiff, gram_mass, MODES, PURIFY)
        directions = jnp.dot(coefficients[MODES:].T, basis[MODES:], precision=PRECISE)
        stiff_directions = jnp.dot(coefficients[MODES:].T, stiff_basis[MODES:], precision=PRECISE)
        modes_now = jnp.dot(coefficients.T, basis, precision=PRECISE)
        stiff_modes = jnp.dot(coefficients.T, stiff_basis, precision=PRECISE)
    weight = mass.shape[0] * lax.axis_size(ROW) / MODES
    mass_density = weight * mass * jnp.sum(modes_now * modes_now, axis=0)
    energy_density = weight * jnp.sum(modes_now * stiff_modes, axis=0)
    return (mass_density, energy_density)


def solution(mesh):
    torus = Mesh(
        mesh.devices.reshape(mesh.shape["sub"], 8, 8, 2), ("sub", "row_0", "row_1", "row_2")
    )
    return jax.shard_map(
        local,
        mesh=torus,
        in_specs=(
            P(SUB_ROW, None, None),
            P(SUB_ROW, None, None, None),
            P(SUB_ROW, None),
            P(SUB_ROW),
            P(None, SUB_ROW),
        ),
        out_specs=(P(SUB_ROW), P(SUB_ROW)),
        check_vma=False,
    )
```

profile of v0, /device:TPU:513, one launch (start us, length us, event | category | flops | bytes accessed | tf_op | source)
XLA Modules:
  0.0 1041.2 jit_solution(16284260710776054212)
XLA Ops:
  8.9 4.6 collective-permute-start
  19.0 19.7 %collective-permute-start.1 = (f32[32,512]{1,0:T(8,128)}, f32[32,512]{1,0:T(8,128)}, u32[]{:S(2)}, u32[]{:S(2)}) collective-permute-start(f32[32,512]{1,0:T(8,128)} %copy_bitcast_fusion.10), channel_id=1, source_target_pairs={{1,0},{2,1},{3,2},{4,3},{5,4},{6,5},{7,6},{8,7},{9,8},{10,9},{11,1... | collective-permute-start | bytes 196616 | tf_op jit(solution)/shard_map/ppermute | solution.py:19
  46.2 6.0 copy.58
  60.5 3.6 convolution_bitcast_fusion.8
  67.1 20.2 %all-reduce.7 = (f32[32,32]{1,0:T(8,128)S(1)}, f32[32,32]{1,0:T(8,128)S(1)}) all-reduce(f32[32,32]{1,0:T(8,128)S(1)} %fusion.60, f32[32,32]{1,0:T(8,128)S(1)} %convolution_bitcast_fusion.9), channel_id=1, replica_groups=mesh['sub'=2,'row_0'=8,'row_1'=8,'row_2'=2] {'row_0'}, use_global_device_ids=true, to_apply=%region_0.1 | all-reduce | flops 2048 | bytes 16384 | tf_op jit(solution)/shard_map/psum | solution.py:24
  87.3 20.3 %all-reduce.3 = (f32[32,32]{1,0:T(8,128)S(1)}, f32[32,32]{1,0:T(8,128)S(1)}) all-reduce(f32[32,32]{1,0:T(8,128)S(1)} %get-tuple-element.143, f32[32,32]{1,0:T(8,128)S(1)} %get-tuple-element.144), channel_id=1, replica_groups=mesh['sub'=2,'row_0'=8,'row_1'=8,'row_2'=2] {'row_1'}, use_global_device_ids=true, to_apply=%region_1.2 | all-reduce | flops 2048 | bytes 16384 | tf_op jit(solution)/shard_map/psum | solution.py:24
  107.6 16.7 %all-reduce.11 = (f32[32,32]{1,0:T(8,128)S(1)}, f32[32,32]{1,0:T(8,128)S(1)}) all-reduce(f32[32,32]{1,0:T(8,128)S(1)} %get-tuple-element.135, f32[32,32]{1,0:T(8,128)S(1)} %get-tuple-element.136), channel_id=1, replica_groups=mesh['sub'=2,'row_0'=8,'row_1'=8,'row_2'=2] {'row_2'}, use_global_device_ids=true, to_apply=%region_2.3 | all-reduce | flops 2048 | bytes 16384 | tf_op jit(solution)/shard_map/psum | solution.py:24
  138.0 2.9 fusion.74
  154.5 4.6 fusion.17
  161.2 20.8 %all-reduce.6 = (f32[64,64]{1,0:T(8,128)S(1)}, f32[64,64]{1,0:T(8,128)S(1)}) all-reduce(f32[64,64]{1,0:T(8,128)S(1)} %fusion.35, f32[64,64]{1,0:T(8,128)S(1)} %fusion.49), channel_id=1, replica_groups=mesh['sub'=2,'row_0'=8,'row_1'=8,'row_2'=2] {'row_0'}, use_global_device_ids=true, to_apply=%region_8.11 | all-reduce | flops 8192 | bytes 65536 | tf_op jit(solution)/shard_map/psum | solution.py:24
  182.0 23.7 %all-reduce.2 = (f32[64,64]{1,0:T(8,128)S(1)}, f32[64,64]{1,0:T(8,128)}) all-reduce(f32[64,64]{1,0:T(8,128)S(1)} %get-tuple-element.141, f32[64,64]{1,0:T(8,128)S(1)} %get-tuple-element.142), channel_id=1, replica_groups=mesh['sub'=2,'row_0'=8,'row_1'=8,'row_2'=2] {'row_1'}, use_global_device_ids=true, to_apply=%region_9.12 | all-reduce | flops 8192 | bytes 65536 | tf_op jit(solution)/shard_map/psum | solution.py:24
  205.6 19.7 %all-reduce.10 = (f32[64,64]{1,0:T(8,128)S(1)}, f32[64,64]{1,0:T(8,128)S(1)}) all-reduce(f32[64,64]{1,0:T(8,128)S(1)} %get-tuple-element.133, f32[64,64]{1,0:T(8,128)} %get-tuple-element.134), channel_id=1, replica_groups=mesh['sub'=2,'row_0'=8,'row_1'=8,'row_2'=2] {'row_2'}, use_global_device_ids=true, to_apply=%region_10.13 | all-reduce | flops 8192 | bytes 65536 | tf_op jit(solution)/shard_map/psum | solution.py:24
  228.3 5.8 cholesky.60
  235.6 4.9 custom-call.22
  245.7 81.9 %while.34 = (s32[]{:T(128)}, f32[64,64]{1,0:T(8,128)S(1)}, s32[]{:T(128)}, f32[]{:T(128)}, f32[]{:T(128)}, /*index=5*/f32[]{:T(128)}, f32[]{:T(128)}, f32[]{:T(128)}) while((s32[]{:T(128)}, f32[64,64]{1,0:T(8,128)S(1)}, s32[]{:T(128)}, f32[]{:T(128)}, f32[]{:T(128)}, /*index=5*/f32[]{:T(128)}, f32[]{:T(128)}, f32[]{:T(128)}) %tuple.100), condition=%wide.region_23.26_spmd, body=%wide.region_20.25_spmd.sunk | while | flops 6352909 | bytes 147713 | solution.py:80
  341.7 3.0 fusion.71
  359.4 4.6 fusion.14
  367.2 75.7 %all-reduce.25.cloned.1.call-done = (f32[96,96]{1,0:T(8,128)}, f32[96,96]{1,0:T(8,128)}) async-done(((f32[96,96]{1,0:T(8,128)}, f32[96,96]{1,0:T(8,128)}), (f32[96,96]{1,0:T(8,128)}, f32[96,96]{1,0:T(8,128)})) %all-reduce.25.cloned.1.call-update) | async-done | bytes 73744 | tf_op jit(solution)/shard_map/psum | solution.py:24
  443.1 75.6 %all-reduce.21.cloned.1.call-done = (f32[96,96]{1,0:T(8,128)}, f32[96,96]{1,0:T(8,128)}) async-done(((f32[96,96]{1,0:T(8,128)}, f32[96,96]{1,0:T(8,128)}), (f32[96,96]{1,0:T(8,128)}, f32[96,96]{1,0:T(8,128)})) %all-reduce.21.cloned.1.call-update) | async-done | bytes 73744 | tf_op jit(solution)/shard_map/psum | solution.py:24
  518.8 38.9 %all-reduce.29.cloned.1.call-done = (f32[96,96]{1,0:T(8,128)}, f32[96,96]{1,0:T(8,128)}) async-done(((f32[96,96]{1,0:T(8,128)}, f32[96,96]{1,0:T(8,128)}), (f32[96,96]{1,0:T(8,128)}, f32[96,96]{1,0:T(8,128)})) %all-reduce.29.cloned.1.call-update) | async-done | bytes 73744 | tf_op jit(solution)/shard_map/psum | solution.py:24
  561.8 8.8 cholesky.205
  571.9 7.4 custom-call.45
  586.0 89.0 %while.35 = (s32[]{:T(128)}, f32[96,96]{1,0:T(8,128)S(1)}, s32[]{:T(128)}, f32[]{:T(128)}, f32[]{:T(128)}, /*index=5*/f32[]{:T(128)}, f32[]{:T(128)}, f32[]{:T(128)}) while((s32[]{:T(128)}, f32[96,96]{1,0:T(8,128)S(1)}, s32[]{:T(128)}, f32[]{:T(128)}, f32[]{:T(128)}, /*index=5*/f32[]{:T(128)}, f32[]{:T(128)}, f32[]{:T(128)}) %tuple.103), condition=%wide.region_39.44_spmd, body=%wide.region_36.43_spmd.sunk | while | flops 21371904 | bytes 332033 | solution.py:80
  676.0 3.6 cholesky.216
  691.3 3.0 fusion.68
  709.9 4.6 fusion.11
  717.6 73.0 %all-reduce.23.cloned.1.call-done = (f32[96,96]{1,0:T(8,128)}, f32[96,96]{1,0:T(8,128)}) async-done(((f32[96,96]{1,0:T(8,128)}, f32[96,96]{1,0:T(8,128)}), (f32[96,96]{1,0:T(8,128)}, f32[96,96]{1,0:T(8,128)})) %all-reduce.23.cloned.1.call-update) | async-done | bytes 73744 | tf_op jit(solution)/shard_map/psum | solution.py:24
  791.1 75.2 %all-reduce.19.cloned.1.call-done = (f32[96,96]{1,0:T(8,128)}, f32[96,96]{1,0:T(8,128)}) async-done(((f32[96,96]{1,0:T(8,128)}, f32[96,96]{1,0:T(8,128)}), (f32[96,96]{1,0:T(8,128)}, f32[96,96]{1,0:T(8,128)})) %all-reduce.19.cloned.1.call-update) | async-done | bytes 73744 | tf_op jit(solution)/shard_map/psum | solution.py:24
  866.4 38.8 %all-reduce.27.cloned.1.call-done = (f32[96,96]{1,0:T(8,128)}, f32[96,96]{1,0:T(8,128)}) async-done(((f32[96,96]{1,0:T(8,128)}, f32[96,96]{1,0:T(8,128)}), (f32[96,96]{1,0:T(8,128)}, f32[96,96]{1,0:T(8,128)})) %all-reduce.27.cloned.1.call-update) | async-done | bytes 73744 | tf_op jit(solution)/shard_map/psum | solution.py:24
  909.8 9.6 cholesky.227
  920.7 8.0 custom-call.47
  937.8 83.4 %while.36 = (s32[]{:T(128)}, f32[96,96]{1,0:T(8,128)S(1)}, s32[]{:T(128)}, f32[]{:T(128)}, f32[]{:T(128)}, /*index=5*/f32[]{:T(128)}, f32[]{:T(128)}, f32[]{:T(128)}) while((s32[]{:T(128)}, f32[96,96]{1,0:T(8,128)S(1)}, s32[]{:T(128)}, f32[]{:T(128)}, f32[]{:T(128)}, /*index=5*/f32[]{:T(128)}, f32[]{:T(128)}, f32[]{:T(128)}) %tuple.106), condition=%wide.region_53.59_spmd, body=%wide.region_50.58_spmd.sunk | while | flops 21371904 | bytes 332033 | solution.py:80
  (565 shorter events, 247.0 us)
Async XLA Ops:
  7.2 8.0 copy-start
  7.2 435.7 %all-reduce.25.cloned.1.call-start = ((), (), s32[]{:S(2)}) async-start(), calls=%async_computation.3 | async-start | bytes 196608 | tf_op jit(solution)/shard_map/psum | solution.py:24
  8.9 46.7 %collective-permute-start = (f32[32,512]{1,0:T(8,128)}, f32[32,512]{1,0:T(8,128)}, u32[]{:S(2)}, u32[]{:S(2)}) collective-permute-start(f32[32,512]{1,0:T(8,128)} %slice.181), channel_id=1, source_target_pairs={{0,1},{1,2},{2,3},{3,4},{4,5},{5,6},{6,7},{7,8},{8,9},{9,10},{10,1... | collective-permute-start | bytes 196616 | tf_op jit(solution)/shard_map/ppermute | solution.py:19
  14.2 687.6 %copy-start.37 = (s32[16,3]{0,1:T(4,128)}, s32[16,3]{0,1:T(4,128)S(1)}, u32[]{:S(2)}) copy-start(s32[16,3]{0,1:T(4,128)S(1)} %subtract_add_fusion) | copy-start | bytes 580
  15.2 23.7 %copy-start.2 = (f32[32,2048]{1,0:T(8,128)S(1)}, f32[32,2048]{1,0:T(8,128)}, u32[]{:S(2)}) copy-start(f32[32,2048]{1,0:T(8,128)} %param.31) | copy-start | bytes 786436
  15.2 23.7 %copy-start.38 = (f32[2048]{0:T(1024)S(1)}, f32[2048]{0:T(1024)}, u32[]{:S(2)}) copy-start(f32[2048]{0:T(1024)} %param.30) | copy-start | bytes 24580
  18.3 20.4 %copy-start.22 = (f32[32,128,20]{1,0,2:T(8,128)}, f32[32,128,20]{1,0,2:T(8,128)S(1)}, u32[]{:S(2)}) copy-start(f32[32,128,20]{1,0,2:T(8,128)S(1)} %copy.223) | copy-start | bytes 983044
  19.0 46.2 %collective-permute-start.1 = (f32[32,512]{1,0:T(8,128)}, f32[32,512]{1,0:T(8,128)}, u32[]{:S(2)}, u32[]{:S(2)}) collective-permute-start(f32[32,512]{1,0:T(8,128)} %copy_bitcast_fusion.10), channel_id=1, source_target_pairs={{1,0},{2,1},{3,2},{4,3},{5,4},{6,5},{7,6},{8,7},{9,8},{10,9},{11,1... | collective-permute-start | bytes 196616 | tf_op jit(solution)/shard_map/ppermute | solution.py:19
  55.5 81.0 %copy-start.39 = (f32[16,128]{1,0:T(8,128)}, f32[16,128]{1,0:T(8,128)S(1)}, u32[]{:S(2)}) copy-start(f32[16,128]{1,0:T(8,128)S(1)} %copy.59) | copy-start | bytes 24580
  141.0 9.4 collective-permute-start.2
  148.3 10.8 %collective-permute-start.3 = (f32[32,512]{1,0:T(8,128)}, f32[32,512]{1,0:T(8,128)S(1)}, u32[]{:S(2)}, u32[]{:S(2)}) collective-permute-start(f32[32,512]{1,0:T(8,128)} %copy_bitcast_fusion.9), channel_id=1, source_target_pairs={{1,0},{2,1},{3,2},{4,3},{5,4},{6,5},{7,6},{8,7},{9,8},{10,9},{11,1... | collective-permute-start | bytes 196616 | tf_op jit(solution)/shard_map/ppermute | solution.py:19
  341.7 15.4 %copy-start.3 = (f32[32,2048]{1,0:T(8,128)}, f32[32,2048]{1,0:T(8,128)S(1)}, u32[]{:S(2)}) copy-start(f32[32,2048]{1,0:T(8,128)S(1)} %fusion.1) | copy-start | bytes 786436
  347.2 8.4 copy-start.12
  347.2 9.8 collective-permute-start.4
  353.5 10.5 %collective-permute-start.5 = (f32[32,512]{1,0:T(8,128)}, f32[32,512]{1,0:T(8,128)}, u32[]{:S(2)}, u32[]{:S(2)}) collective-permute-start(f32[32,512]{1,0:T(8,128)} %copy_bitcast_fusion.8), channel_id=1, source_target_pairs={{1,0},{2,1},{3,2},{4,3},{5,4},{6,5},{7,6},{8,7},{9,8},{10,9},{11,1... | collective-permute-start | bytes 196616 | tf_op jit(solution)/shard_map/ppermute | solution.py:19
  367.1 151.6 %all-reduce.21.cloned.1.call-start = ((), (), s32[]{:S(2)}) async-start(), calls=%async_computation.1 | async-start | bytes 196608 | tf_op jit(solution)/shard_map/psum | solution.py:24
  443.0 114.8 %all-reduce.29.cloned.1.call-start = ((), (), s32[]{:S(2)}) async-start(), calls=%async_computation.5 | async-start | bytes 196608 | tf_op jit(solution)/shard_map/psum | solution.py:24
  518.8 271.9 %all-reduce.23.cloned.1.call-start = ((), (), s32[]{:S(2)}) async-start(), calls=%async_computation.2 | async-start | bytes 196608 | tf_op jit(solution)/shard_map/psum | solution.py:24
  560.8 25.3 %copy-start.42 = (f32[96]{0:T(128)}, f32[96]{0:T(128)S(1)}, u32[]{:S(2)}) copy-start(f32[96]{0:T(128)S(1)} %get-tuple-element.165) | copy-start | bytes 1156
  675.0 21.4 %copy-start.5 = (f32[32,2048]{1,0:T(8,128)S(1)}, f32[32,2048]{1,0:T(8,128)}, u32[]{:S(2)}) copy-start(f32[32,2048]{1,0:T(8,128)} %copy-done.3) | copy-start | bytes 786436
  691.3 16.1 %copy-start.8 = (f32[32,2048]{1,0:T(8,128)}, f32[32,2048]{1,0:T(8,128)S(1)}, u32[]{:S(2)}) copy-start(f32[32,2048]{1,0:T(8,128)S(1)} %fusion) | copy-start | bytes 786436
  696.9 9.1 copy-start.28
  696.9 10.5 %collective-permute-start.6 = (f32[32,512]{1,0:T(8,128)S(1)}, f32[32,512]{1,0:T(8,128)S(1)}, u32[]{:S(2)}, u32[]{:S(2)}) collective-permute-start(f32[32,512]{1,0:T(8,128)S(1)} %slice.231), channel_id=1, source_target_pairs={{0,1},{1,2},{2,3},{3,4},{4,5},{5,6},{6,7},{7,8},{8,9},{9,10},{10,1... | collective-permute-start | bytes 196616 | tf_op jit(solution)/shard_map/ppermute | solution.py:19
  704.0 10.5 %collective-permute-start.7 = (f32[32,512]{1,0:T(8,128)}, f32[32,512]{1,0:T(8,128)}, u32[]{:S(2)}, u32[]{:S(2)}) collective-permute-start(f32[32,512]{1,0:T(8,128)} %copy_bitcast_fusion.7), channel_id=1, source_target_pairs={{1,0},{2,1},{3,2},{4,3},{5,4},{6,5},{7,6},{8,7},{9,8},{10,9},{11,1... | collective-permute-start | bytes 196616 | tf_op jit(solution)/shard_map/ppermute | solution.py:19
  708.2 7.9 copy-start.9
  708.2 7.9 copy-start.24
  708.2 7.9 copy-start.29
  708.2 7.9 copy-start.31
  708.2 7.9 copy-start.33
  717.6 148.7 %all-reduce.19.cloned.1.call-start = ((), (), s32[]{:S(2)}) async-start(), calls=%async_computation | async-start | bytes 196608 | tf_op jit(solution)/shard_map/psum | solution.py:24
  790.7 114.5 %all-reduce.27.cloned.1.call-start = ((), (), s32[]{:S(2)}) async-start(), calls=%async_computation.4 | async-start | bytes 196608 | tf_op jit(solution)/shard_map/psum | solution.py:24
  908.2 29.5 %copy-start.40 = (f32[96]{0:T(128)}, f32[96]{0:T(128)S(1)}, u32[]{:S(2)}) copy-start(f32[96]{0:T(128)S(1)} %get-tuple-element.163) | copy-start | bytes 1156
  (26 other events, 99.1 us)
Sparse Core Ops, SparseCore 0:
  367.2 75.6 all-reduce.24
  445.4 73.2 all-reduce.20
  521.3 36.3 all-reduce.28
  717.7 72.9 all-reduce.22
  793.0 73.2 all-reduce.18
  868.8 36.3 all-reduce.26
where the time goes:
time: 1050 us; the launch traced here: 1040 us
  waiting for transfers between devices  378 us (36%)
  matrix products  173 us (16%)
  loops' own time  168 us (16%)
  blocking collectives  121 us (12%)
  other arithmetic  101 us (10%)
  local copies, waits for them, and re-layouts  39.7 us (4%)
  starting transfers between devices  38.4 us (4%)
  between operations  22.1 us (2%)
    psum x6, waiting for transfers between devices, one_axis_at_a_time(): value = lax.psum(value, axis)  377 us
    another operation x3, loops' own time, purify(): return lax.fori_loop(0, steps_count, purify_step, initial)  168 us
    psum x6, blocking collectives, one_axis_at_a_time(): value = lax.psum(value, axis)  121 us
    dot_general x84, matrix products, purify_step(): cube = jnp.dot(square, density, precision=PRECISE)  69.6 us
    ppermute x8, starting transfers between devices, from_behind(): lax.ppermute(value, axis, [(source, source + steps) for source in range(i...  37.8 us
    another operation x12, other arithmetic, ritz_basis(): factor_low = jnp.linalg.cholesky(mass_scaled)  30 us
    another operation x8, other arithmetic, ritz_basis(): lax.linalg.triangular_solve(factor_low, identity, left_side=True, lower=T...  25.2 us
  transfers between devices with their start and end apart: 14, of which 6 were waited for; matrix products, arithmetic and copies ran while one was open for 7% of the time, Pallas kernels for 0%

commit v1 on v0

--- a/solution.py
+++ b/solution.py
@@ -21,7 +21,7 @@
 
 def one_axis_at_a_time(value, axes):
     for axis in axes:
-        value = lax.psum(value, axis)
+        value = jnp.sum(lax.all_gather(value, axis), axis=0)
     return value
 
 

time: 1050 us -> 998 us (0.950)
  waiting for transfers between devices: 378 us -> 0.03 us
  blocking collectives: 121 us -> 450 us
  other arithmetic: 101 us -> 123 us
  between operations: 22.1 us -> 8.3 us
    all_gather x0 -> x24, blocking collectives: none -> 450 us  [one_axis_at_a_time(): value = jnp.sum(lax.all_gather(value, axis), axis=0)]
    psum x6 -> x0, waiting for transfers between devices: 377 us -> none  [one_axis_at_a_time(): value = lax.psum(value, axis)]
    psum x6 -> x0, blocking collectives: 121 us -> none  [one_axis_at_a_time(): value = lax.psum(value, axis)]
    reduce_sum x0 -> x24, other arithmetic: none -> 16.1 us  [one_axis_at_a_time(): value = jnp.sum(lax.all_gather(value, axis), axis=0)]
  transfers between devices with their start and end apart: 14 -> 8, of which waited for: 6 -> 0; matrix products, arithmetic and copies ran while one was open for 7% -> 15% of each run, Pallas kernels for 0% -> 0%
where the time goes in v1:
time: 998 us; the launch traced here: 988 us
  blocking collectives  450 us (45%)
  matrix products  171 us (17%)
  loops' own time  159 us (16%)
  other arithmetic  123 us (12%)
  starting transfers between devices  39.3 us (4%)
  local copies, waits for them, and re-layouts  37.8 us (4%)
    all_gather x24, blocking collectives, one_axis_at_a_time(): value = jnp.sum(lax.all_gather(value, axis), axis=0)  450 us
    another operation x3, loops' own time, purify(): return lax.fori_loop(0, steps_count, purify_step, initial)  159 us
    dot_general x84, matrix products, purify_step(): cube = jnp.dot(square, density, precision=PRECISE)  67.9 us
    ppermute x8, starting transfers between devices, from_behind(): lax.ppermute(value, axis, [(source, source + steps) for source in range(i...  39.3 us
    another operation x12, other arithmetic, ritz_basis(): factor_low = jnp.linalg.cholesky(mass_scaled)  30.6 us
    another operation x8, other arithmetic, ritz_basis(): lax.linalg.triangular_solve(factor_low, identity, left_side=True, lower=T...  25.2 us
  transfers between devices with their start and end apart: 8, of which 0 were waited for; matrix products, arithmetic and copies ran while one was open for 15% of the time, Pallas kernels for 0%

profile of v1, /device:TPU:513, one launch (start us, length us, event | category | flops | bytes accessed | tf_op | source)
XLA Modules:
  0.0 987.8 jit_solution(11650982703895137587)
XLA Ops:
  12.4 19.7 %collective-permute-start.1 = (f32[32,512]{1,0:T(8,128)}, f32[32,512]{1,0:T(8,128)}, u32[]{:S(2)}, u32[]{:S(2)}) collective-permute-start(f32[32,512]{1,0:T(8,128)} %copy_bitcast_fusion.10), channel_id=1, source_target_pairs={{1,0},{2,1},{3,2},{4,3},{5,4},{6,5},{7,6},{8,7},{9,8},{10,9},{11,1... | collective-permute-start | bytes 196616 | tf_op jit(solution)/shard_map/ppermute | solution.py:19
  32.6 20.6 %all-gather = f32[256,32]{1,0:T(8,128)} all-gather(f32[32,32]{1,0:T(8,128)S(1)} %fusion.48), channel_id=2, replica_groups=mesh['sub'=2,'row_0'=8,'row_1'=8,'row_2'=2] {'row_0'}, dimensions={0}, use_global_device_ids=true | all-gather | bytes 36864 | tf_op jit(solution)/shard_map/all_gather | solution.py:24
  54.1 20.3 %all-gather.1 = f32[256,32]{1,0:T(8,128)} all-gather(f32[32,32]{1,0:T(8,128)S(1)} %reduce_sum.332), channel_id=3, replica_groups=mesh['sub'=2,'row_0'=8,'row_1'=8,'row_2'=2] {'row_1'}, dimensions={0}, use_global_device_ids=true | all-gather | bytes 36864 | tf_op jit(solution)/shard_map/all_gather | solution.py:24
  75.3 13.8 %all-gather.2 = f32[64,32]{1,0:T(8,128)S(1)} all-gather(f32[32,32]{1,0:T(8,128)S(1)} %reduce_sum.333), channel_id=4, replica_groups=mesh['sub'=2,'row_0'=8,'row_1'=8,'row_2'=2] {'row_2'}, dimensions={0}, use_global_device_ids=true | all-gather | bytes 12288 | tf_op jit(solution)/shard_map/all_gather | solution.py:24
  125.9 18.3 %all-gather.3 = f32[256,32]{1,0:T(8,128)S(1)} all-gather(f32[32,32]{1,0:T(8,128)S(1)} %copy.286), channel_id=5, replica_groups=mesh['sub'=2,'row_0'=8,'row_1'=8,'row_2'=2] {'row_0'}, dimensions={0}, use_global_device_ids=true | all-gather | bytes 36864 | tf_op jit(solution)/shard_map/all_gather | solution.py:24
  144.2 18.3 %all-gather.4 = f32[256,32]{1,0:T(8,128)S(1)} all-gather(f32[32,32]{1,0:T(8,128)S(1)} %reduce_sum.335), channel_id=6, replica_groups=mesh['sub'=2,'row_0'=8,'row_1'=8,'row_2'=2] {'row_1'}, dimensions={0}, use_global_device_ids=true | all-gather | bytes 36864 | tf_op jit(solution)/shard_map/all_gather | solution.py:24
  162.5 14.7 %all-gather.5 = f32[64,32]{1,0:T(8,128)S(1)} all-gather(f32[32,32]{1,0:T(8,128)S(1)} %reduce_sum.336), channel_id=7, replica_groups=mesh['sub'=2,'row_0'=8,'row_1'=8,'row_2'=2] {'row_2'}, dimensions={0}, use_global_device_ids=true | all-gather | bytes 12288 | tf_op jit(solution)/shard_map/all_gather | solution.py:24
  194.3 20.6 %all-gather.6 = f32[512,64]{1,0:T(8,128)} all-gather(f32[64,64]{1,0:T(8,128)S(1)} %fusion.27), channel_id=8, replica_groups=mesh['sub'=2,'row_0'=8,'row_1'=8,'row_2'=2] {'row_0'}, dimensions={0}, use_global_device_ids=true | all-gather | bytes 147456 | tf_op jit(solution)/shard_map/all_gather | solution.py:24
  215.8 20.9 %all-gather.7 = f32[512,64]{1,0:T(8,128)} all-gather(f32[64,64]{1,0:T(8,128)S(1)} %reduce_sum.338), channel_id=9, replica_groups=mesh['sub'=2,'row_0'=8,'row_1'=8,'row_2'=2] {'row_1'}, dimensions={0}, use_global_device_ids=true | all-gather | bytes 147456 | tf_op jit(solution)/shard_map/all_gather | solution.py:24
  237.7 15.8 %all-gather.8 = f32[128,64]{1,0:T(8,128)S(1)} all-gather(f32[64,64]{1,0:T(8,128)S(1)} %reduce_sum.339), channel_id=10, replica_groups=mesh['sub'=2,'row_0'=8,'row_1'=8,'row_2'=2] {'row_2'}, dimensions={0}, use_global_device_ids=true | all-gather | bytes 49152 | tf_op jit(solution)/shard_map/all_gather | solution.py:24
  278.5 20.4 %all-gather.9 = f32[512,64]{1,0:T(8,128)} all-gather(f32[64,64]{1,0:T(8,128)S(1)} %fusion.41), channel_id=11, replica_groups=mesh['sub'=2,'row_0'=8,'row_1'=8,'row_2'=2] {'row_0'}, dimensions={0}, use_global_device_ids=true | all-gather | bytes 147456 | tf_op jit(solution)/shard_map/all_gather | solution.py:24
  299.9 20.5 %all-gather.10 = f32[512,64]{1,0:T(8,128)} all-gather(f32[64,64]{1,0:T(8,128)S(1)} %reduce_sum.341), channel_id=12, replica_groups=mesh['sub'=2,'row_0'=8,'row_1'=8,'row_2'=2] {'row_1'}, dimensions={0}, use_global_device_ids=true | all-gather | bytes 147456 | tf_op jit(solution)/shard_map/all_gather | solution.py:24
  321.4 15.0 %all-gather.11 = f32[128,64]{1,0:T(8,128)S(1)} all-gather(f32[64,64]{1,0:T(8,128)S(1)} %reduce_sum.342), channel_id=13, replica_groups=mesh['sub'=2,'row_0'=8,'row_1'=8,'row_2'=2] {'row_2'}, dimensions={0}, use_global_device_ids=true | all-gather | bytes 49152 | tf_op jit(solution)/shard_map/all_gather | solution.py:24
  341.2 81.4 %while.34 = (s32[]{:T(128)}, f32[64,64]{1,0:T(8,128)S(1)}, s32[]{:T(128)}, f32[]{:T(128)}, f32[]{:T(128)}, /*index=5*/f32[]{:T(128)}, f32[]{:T(128)}, f32[]{:T(128)}) while((s32[]{:T(128)}, f32[64,64]{1,0:T(8,128)S(1)}, s32[]{:T(128)}, f32[]{:T(128)}, f32[]{:T(128)}, /*index=5*/f32[]{:T(128)}, f32[]{:T(128)}, f32[]{:T(128)}) %tuple.108), condition=%wide.region_23.26_spmd, body=%wide.region_20.25_spmd.sunk | while | flops 6352909 | bytes 147713 | solution.py:80
  452.7 20.8 %all-gather.12 = f32[768,96]{1,0:T(8,128)} all-gather(f32[96,96]{1,0:T(8,128)S(1)} %fusion.5), channel_id=14, replica_groups=mesh['sub'=2,'row_0'=8,'row_1'=8,'row_2'=2] {'row_0'}, dimensions={0}, use_global_device_ids=true | all-gather | bytes 331776 | tf_op jit(solution)/shard_map/all_gather | solution.py:24
  474.5 21.2 %all-gather.13 = f32[768,96]{1,0:T(8,128)} all-gather(f32[96,96]{1,0:T(8,128)S(1)} %reduce_sum.346), channel_id=15, replica_groups=mesh['sub'=2,'row_0'=8,'row_1'=8,'row_2'=2] {'row_1'}, dimensions={0}, use_global_device_ids=true | all-gather | bytes 331776 | tf_op jit(solution)/shard_map/all_gather | solution.py:24
  496.7 18.1 %all-gather.14 = f32[192,96]{1,0:T(8,128)} all-gather(f32[96,96]{1,0:T(8,128)S(1)} %reduce_sum.347), channel_id=16, replica_groups=mesh['sub'=2,'row_0'=8,'row_1'=8,'row_2'=2] {'row_2'}, dimensions={0}, use_global_device_ids=true | all-gather | bytes 110592 | tf_op jit(solution)/shard_map/all_gather | solution.py:24
  520.2 9.6 cholesky.205
  531.1 7.4 custom-call.45
  550.7 19.1 %all-gather.15 = f32[768,96]{1,0:T(8,128)S(1)} all-gather(f32[96,96]{1,0:T(8,128)S(1)} %fusion.31), channel_id=17, replica_groups=mesh['sub'=2,'row_0'=8,'row_1'=8,'row_2'=2] {'row_0'}, dimensions={0}, use_global_device_ids=true | all-gather | bytes 331776 | tf_op jit(solution)/shard_map/all_gather | solution.py:24
  570.5 19.3 %all-gather.16 = f32[768,96]{1,0:T(8,128)S(1)} all-gather(f32[96,96]{1,0:T(8,128)} %reduce_sum.349), channel_id=18, replica_groups=mesh['sub'=2,'row_0'=8,'row_1'=8,'row_2'=2] {'row_1'}, dimensions={0}, use_global_device_ids=true | all-gather | bytes 331776 | tf_op jit(solution)/shard_map/all_gather | solution.py:24
  590.5 14.2 %all-gather.17 = f32[192,96]{1,0:T(8,128)S(1)} all-gather(f32[96,96]{1,0:T(8,128)} %reduce_sum.350), channel_id=19, replica_groups=mesh['sub'=2,'row_0'=8,'row_1'=8,'row_2'=2] {'row_2'}, dimensions={0}, use_global_device_ids=true | all-gather | bytes 110592 | tf_op jit(solution)/shard_map/all_gather | solution.py:24
  611.1 78.1 %while.35 = (s32[]{:T(128)}, f32[96,96]{1,0:T(8,128)S(1)}, s32[]{:T(128)}, f32[]{:T(128)}, f32[]{:T(128)}, /*index=5*/f32[]{:T(128)}, f32[]{:T(128)}, f32[]{:T(128)}) while((s32[]{:T(128)}, f32[96,96]{1,0:T(8,128)S(1)}, s32[]{:T(128)}, f32[]{:T(128)}, f32[]{:T(128)}, /*index=5*/f32[]{:T(128)}, f32[]{:T(128)}, f32[]{:T(128)}) %tuple.111), condition=%wide.region_39.44_spmd, body=%wide.region_36.43_spmd.sunk | while | flops 21371904 | bytes 332033 | solution.py:80
  724.6 21.2 %all-gather.18 = f32[768,96]{1,0:T(8,128)} all-gather(f32[96,96]{1,0:T(8,128)S(1)} %fusion.3), channel_id=20, replica_groups=mesh['sub'=2,'row_0'=8,'row_1'=8,'row_2'=2] {'row_0'}, dimensions={0}, use_global_device_ids=true | all-gather | bytes 331776 | tf_op jit(solution)/shard_map/all_gather | solution.py:24
  746.8 21.1 %all-gather.19 = f32[768,96]{1,0:T(8,128)} all-gather(f32[96,96]{1,0:T(8,128)S(1)} %reduce_sum.354), channel_id=21, replica_groups=mesh['sub'=2,'row_0'=8,'row_1'=8,'row_2'=2] {'row_1'}, dimensions={0}, use_global_device_ids=true | all-gather | bytes 331776 | tf_op jit(solution)/shard_map/all_gather | solution.py:24
  768.9 18.4 %all-gather.20 = f32[192,96]{1,0:T(8,128)} all-gather(f32[96,96]{1,0:T(8,128)S(1)} %reduce_sum.355), channel_id=22, replica_groups=mesh['sub'=2,'row_0'=8,'row_1'=8,'row_2'=2] {'row_2'}, dimensions={0}, use_global_device_ids=true | all-gather | bytes 110592 | tf_op jit(solution)/shard_map/all_gather | solution.py:24
  792.7 9.6 cholesky.227
  803.6 8.0 custom-call.47
  824.0 21.3 %all-gather.21 = f32[768,96]{1,0:T(8,128)} all-gather(f32[96,96]{1,0:T(8,128)S(1)} %fusion.29), channel_id=23, replica_groups=mesh['sub'=2,'row_0'=8,'row_1'=8,'row_2'=2] {'row_0'}, dimensions={0}, use_global_device_ids=true | all-gather | bytes 331776 | tf_op jit(solution)/shard_map/all_gather | solution.py:24
  846.4 20.9 %all-gather.22 = f32[768,96]{1,0:T(8,128)} all-gather(f32[96,96]{1,0:T(8,128)S(1)} %reduce_sum.357), channel_id=24, replica_groups=mesh['sub'=2,'row_0'=8,'row_1'=8,'row_2'=2] {'row_1'}, dimensions={0}, use_global_device_ids=true | all-gather | bytes 331776 | tf_op jit(solution)/shard_map/all_gather | solution.py:24
  868.3 14.6 %all-gather.23 = f32[192,96]{1,0:T(8,128)} all-gather(f32[96,96]{1,0:T(8,128)S(1)} %reduce_sum.358), channel_id=25, replica_groups=mesh['sub'=2,'row_0'=8,'row_1'=8,'row_2'=2] {'row_2'}, dimensions={0}, use_global_device_ids=true | all-gather | bytes 110592 | tf_op jit(solution)/shard_map/all_gather | solution.py:24
  891.6 83.4 %while.36 = (s32[]{:T(128)}, f32[96,96]{1,0:T(8,128)S(1)}, s32[]{:T(128)}, f32[]{:T(128)}, f32[]{:T(128)}, /*index=5*/f32[]{:T(128)}, f32[]{:T(128)}, f32[]{:T(128)}) while((s32[]{:T(128)}, f32[96,96]{1,0:T(8,128)S(1)}, s32[]{:T(128)}, f32[]{:T(128)}, f32[]{:T(128)}, /*index=5*/f32[]{:T(128)}, f32[]{:T(128)}, f32[]{:T(128)}) %tuple.114), condition=%wide.region_53.59_spmd, body=%wide.region_50.58_spmd.sunk | while | flops 21371904 | bytes 332033 | solution.py:80
  (586 shorter events, 317.1 us)
Async XLA Ops:
  0.6 7.9 copy-start
  2.3 111.6 %collective-permute-start = (f32[32,512]{1,0:T(8,128)}, f32[32,512]{1,0:T(8,128)}, u32[]{:S(2)}, u32[]{:S(2)}) collective-permute-start(f32[32,512]{1,0:T(8,128)} %slice.181), channel_id=1, source_target_pairs={{0,1},{1,2},{2,3},{3,4},{4,5},{5,6},{6,7},{7,8},{8,9},{9,10},{10,1... | collective-permute-start | bytes 196616 | tf_op jit(solution)/shard_map/ppermute | solution.py:19
  7.5 710.7 %copy-start.34 = (s32[16,3]{0,1:T(4,128)}, s32[16,3]{0,1:T(4,128)S(1)}, u32[]{:S(2)}) copy-start(s32[16,3]{0,1:T(4,128)S(1)} %subtract_add_fusion) | copy-start | bytes 580
  8.5 23.7 %copy-start.2 = (f32[32,2048]{1,0:T(8,128)S(1)}, f32[32,2048]{1,0:T(8,128)}, u32[]{:S(2)}) copy-start(f32[32,2048]{1,0:T(8,128)} %param.31) | copy-start | bytes 786436
  8.6 23.7 %copy-start.36 = (f32[2048]{0:T(1024)S(1)}, f32[2048]{0:T(1024)}, u32[]{:S(2)}) copy-start(f32[2048]{0:T(1024)} %param.30) | copy-start | bytes 24580
  11.7 20.6 %copy-start.20 = (f32[32,128,20]{1,0,2:T(8,128)}, f32[32,128,20]{1,0,2:T(8,128)S(1)}, u32[]{:S(2)}) copy-start(f32[32,128,20]{1,0,2:T(8,128)S(1)} %copy.453) | copy-start | bytes 983044
  12.4 111.1 %collective-permute-start.1 = (f32[32,512]{1,0:T(8,128)}, f32[32,512]{1,0:T(8,128)}, u32[]{:S(2)}, u32[]{:S(2)}) collective-permute-start(f32[32,512]{1,0:T(8,128)} %copy_bitcast_fusion.10), channel_id=1, source_target_pairs={{1,0},{2,1},{3,2},{4,3},{5,4},{6,5},{7,6},{8,7},{9,8},{10,9},{11,1... | collective-permute-start | bytes 196616 | tf_op jit(solution)/shard_map/ppermute | solution.py:19
  122.4 55.7 %copy-start.39 = (f32[16,128]{1,0:T(8,128)S(1)}, f32[16,128]{1,0:T(8,128)}, u32[]{:S(2)}) copy-start(f32[16,128]{1,0:T(8,128)} %copy.296) | copy-start | bytes 24580
  184.8 82.5 %collective-permute-start.2 = (f32[32,512]{1,0:T(8,128)}, f32[32,512]{1,0:T(8,128)}, u32[]{:S(2)}, u32[]{:S(2)}) collective-permute-start(f32[32,512]{1,0:T(8,128)} %slice.221), channel_id=1, source_target_pairs={{0,1},{1,2},{2,3},{3,4},{4,5},{5,6},{6,7},{7,8},{8,9},{9,10},{10,1... | collective-permute-start | bytes 196616 | tf_op jit(solution)/shard_map/ppermute | solution.py:19
  191.2 85.7 %collective-permute-start.3 = (f32[32,512]{1,0:T(8,128)}, f32[32,512]{1,0:T(8,128)}, u32[]{:S(2)}, u32[]{:S(2)}) collective-permute-start(f32[32,512]{1,0:T(8,128)} %copy_bitcast_fusion.9), channel_id=1, source_target_pairs={{1,0},{2,1},{3,2},{4,3},{5,4},{6,5},{7,6},{8,7},{9,8},{10,9},{11,1... | collective-permute-start | bytes 196616 | tf_op jit(solution)/shard_map/ppermute | solution.py:19
  267.3 70.1 %copy-start.33 = (f32[64,64]{1,0:T(8,128)}, f32[64,64]{1,0:T(8,128)S(1)}, u32[]{:S(2)}) copy-start(f32[64,64]{1,0:T(8,128)S(1)} %fusion.121) | copy-start | bytes 49156
  277.8 21.1 %copy-start.16 = (f32[32,2048]{1,0:T(8,128)}, f32[32,2048]{1,0:T(8,128)S(1)}, u32[]{:S(2)}) copy-start(f32[32,2048]{1,0:T(8,128)S(1)} %copy_bitcast_fusion.6) | copy-start | bytes 786436
  436.9 14.9 %copy-start.3 = (f32[32,2048]{1,0:T(8,128)}, f32[32,2048]{1,0:T(8,128)S(1)}, u32[]{:S(2)}) copy-start(f32[32,2048]{1,0:T(8,128)S(1)} %fusion.1) | copy-start | bytes 786436
  443.0 8.8 copy-start.11
  443.0 96.4 %collective-permute-start.4 = (f32[32,512]{1,0:T(8,128)}, f32[32,512]{1,0:T(8,128)}, u32[]{:S(2)}, u32[]{:S(2)}) collective-permute-start(f32[32,512]{1,0:T(8,128)} %slice.226), channel_id=1, source_target_pairs={{0,1},{1,2},{2,3},{3,4},{4,5},{5,6},{6,7},{7,8},{8,9},{9,10},{10,1... | collective-permute-start | bytes 196616 | tf_op jit(solution)/shard_map/ppermute | solution.py:19
  448.7 100.3 %collective-permute-start.5 = (f32[32,512]{1,0:T(8,128)}, f32[32,512]{1,0:T(8,128)}, u32[]{:S(2)}, u32[]{:S(2)}) collective-permute-start(f32[32,512]{1,0:T(8,128)} %copy_bitcast_fusion.8), channel_id=1, source_target_pairs={{1,0},{2,1},{3,2},{4,3},{5,4},{6,5},{7,6},{8,7},{9,8},{10,9},{11,1... | collective-permute-start | bytes 196616 | tf_op jit(solution)/shard_map/ppermute | solution.py:19
  452.6 86.8 %copy-start.4 = (f32[32,2048]{1,0:T(8,128)S(1)}, f32[32,2048]{1,0:T(8,128)}, u32[]{:S(2)}) copy-start(f32[32,2048]{1,0:T(8,128)} %copy-done.3) | copy-start | bytes 786436
  542.8 7.2 copy-start.27
  607.0 99.4 %copy-start.38 = (f32[2048]{0:T(1024)S(1)}, f32[2048]{0:T(1024)}, u32[]{:S(2)}) copy-start(f32[2048]{0:T(1024)} %param.30) | copy-start | bytes 24580
  607.0 99.4 %copy-start.40 = (f32[16,128]{1,0:T(8,128)S(1)}, f32[16,128]{1,0:T(8,128)}, u32[]{:S(2)}) copy-start(f32[16,128]{1,0:T(8,128)} %copy.296) | copy-start | bytes 24580
  689.2 24.5 %copy-start.5 = (f32[32,2048]{1,0:T(8,128)S(1)}, f32[32,2048]{1,0:T(8,128)}, u32[]{:S(2)}) copy-start(f32[32,2048]{1,0:T(8,128)} %copy-done.3) | copy-start | bytes 786436
  706.4 7.3 copy-start.13
  707.9 15.8 %copy-start.7 = (f32[32,2048]{1,0:T(8,128)}, f32[32,2048]{1,0:T(8,128)S(1)}, u32[]{:S(2)}) copy-start(f32[32,2048]{1,0:T(8,128)S(1)} %fusion) | copy-start | bytes 786436
  714.1 9.6 copy-start.23
  714.1 98.5 %collective-permute-start.6 = (f32[32,512]{1,0:T(8,128)}, f32[32,512]{1,0:T(8,128)}, u32[]{:S(2)}, u32[]{:S(2)}) collective-permute-start(f32[32,512]{1,0:T(8,128)} %slice.231), channel_id=1, source_target_pairs={{0,1},{1,2},{2,3},{3,4},{4,5},{5,6},{6,7},{7,8},{8,9},{9,10},{10,1... | collective-permute-start | bytes 196616 | tf_op jit(solution)/shard_map/ppermute | solution.py:19
  716.1 7.6 copy-start.30
  720.5 95.5 %copy-start.35 = (s32[16,3]{0,1:T(4,128)S(1)}, s32[16,3]{0,1:T(4,128)}, u32[]{:S(2)}) copy-start(s32[16,3]{0,1:T(4,128)} %copy-done.34) | copy-start | bytes 580
  720.5 101.7 %collective-permute-start.7 = (f32[32,512]{1,0:T(8,128)}, f32[32,512]{1,0:T(8,128)}, u32[]{:S(2)}, u32[]{:S(2)}) collective-permute-start(f32[32,512]{1,0:T(8,128)} %copy_bitcast_fusion.7), channel_id=1, source_target_pairs={{1,0},{2,1},{3,2},{4,3},{5,4},{6,5},{7,6},{8,7},{9,8},{10,9},{11,1... | collective-permute-start | bytes 196616 | tf_op jit(solution)/shard_map/ppermute | solution.py:19
  724.5 88.1 %copy-start.8 = (f32[32,2048]{1,0:T(8,128)S(1)}, f32[32,2048]{1,0:T(8,128)}, u32[]{:S(2)}) copy-start(f32[32,2048]{1,0:T(8,128)} %copy-done.7) | copy-start | bytes 786436
  791.1 93.5 %copy-start.41 = (f32[96]{0:T(128)}, f32[96]{0:T(128)S(1)}, u32[]{:S(2)}) copy-start(f32[96]{0:T(128)S(1)} %get-tuple-element.155) | copy-start | bytes 1156
  812.6 73.0 %copy-start.32 = (f32[96,96]{1,0:T(8,128)}, f32[96,96]{1,0:T(8,128)S(1)}, u32[]{:S(2)}) copy-start(f32[96,96]{1,0:T(8,128)S(1)} %fusion.81) | copy-start | bytes 110596
  816.0 7.2 copy-start.31
  (19 other events, 90.0 us)
